TPU v7x, 32 devices: a whole 2x2x4 slice. The times are simulated.
32 devices in a mesh: tm: 16 (over z, y, x), col: 2 (over core).
Axes of the slice: x: 2, y: 2, z: 4, core: 2. Of those that a mesh axis runs over, the one named last changes fastest.
Arguments:
- initial_state: float32 [1024], replicated, may hold values from -6 to 6
- coupling: float32 [1024, 1024], replicated, may hold values from -0.1875 to 0.1875
- modulation: float32 [1024, 1024], replicated, may hold values from -0.1875 to 0.1875
- gains: float32 [16, 5], P('tm'), may hold values from -1 to 1
- forcing: float32 [16, 5, 1024], P('tm'), may hold values from -6 to 6
Outputs:
- slab_ends: float32 [16, 1024], P('tm', 'col')
All inputs are finite; a program needn't handle non-finite values.
Results may differ from a plain program's by a relative error of at most 0.0003.
Values sent between devices are 32-bit elements; how exact they have to be, the bound alone decides.
No kernel may reach another device: no remote copies, remote signals or barrier semaphores. Data moves between devices by JAX's collectives and lax.ppermute only.
A program may use at most 128 MiB of HBM per device.

v0:
```python
import jax
import jax.numpy as jnp
from jax import lax
from jax.experimental import pallas as pl
from jax.experimental.pallas import tpu as pltpu
from jax.sharding import PartitionSpec as P

step_size = 0.1
half = jnp.bfloat16
full = jnp.float32
tile = 256
min_cols = 64
spare_rows = 16


def group_span(state_size, time_parts, col_parts):
    span = max(1, state_size // (min_cols * col_parts))
    while span > 1 and (time_parts % span or state_size % (span * col_parts)):
        span -= 1
    return min(span, time_parts)


def split(value):
    high = value.astype(half)
    return high, (value - high.astype(full)).astype(half)


def panel_kernel(state_size, nodes, span, cols):
    rows = cols + spare_rows
    step_count = (nodes - 1) // 2
    blocks = state_size // tile

    def kernel(coupling, modulation, initial, slab_data, panels, base, vary, *splits):
        highs, lows = splits[:3], splits[3:]

        def build(source, target):
            for i in range(blocks):
                for j in range(i, blocks):
                    upper = source[i * tile:(i + 1) * tile, j * tile:(j + 1) * tile]
                    lower = source[j * tile:(j + 1) * tile, i * tile:(i + 1) * tile]
                    target[i * tile:(i + 1) * tile, j * tile:(j + 1) * tile] = lower.T - upper
                    if j > i:
                        target[j * tile:(j + 1) * tile, i * tile:(i + 1) * tile] = upper.T - lower

        build(coupling, base)
        build(modulation, vary)

        def form(slab, node, slot, begin, end):
            gain = slab_data[slab, nodes, node * 128:(node + 1) * 128].reshape(1, 128)
            gain = jnp.concatenate([gain] * (state_size // 128), axis=1)
            for row in range(begin, end, 128):
                value = base[row:row + 128, :] + gain * vary[row:row + 128, :]
                high, low = split(value)
                highs[slot][row:row + 128, :] = high
                lows[slot][row:row + 128, :] = low

        def apply_op(value, slot):
            high, low = split(value)
            both = jnp.concatenate([high, low], axis=0)
            main = jnp.dot(both, highs[slot][...], preferred_element_type=full)
            rest = jnp.dot(high, lows[slot][...], preferred_element_type=full)
            return main[:rows] + main[rows:] + rest

        row_ids = lax.broadcasted_iota(jnp.int32, (rows, state_size), 0)
        col_ids = lax.broadcasted_iota(jnp.int32, (rows, state_size), 1)
        time_index = lax.axis_index("tm")
        member = (time_index % span) * lax.axis_size("col") + lax.axis_index("col")
        start = jnp.where((row_ids + member * cols == col_ids) & (row_ids < cols), 1.0, 0.0)
        weight = jnp.where(time_index < span, 1.0, 0.0)
        start = start + jnp.where(row_ids == rows - 1, weight * initial[...], 0.0)
        is_last = jnp.where(lax.broadcasted_iota(jnp.int32, (rows, 1), 0) == rows - 1, 1.0, 0.0)

        slots = [2 if node == 0 else node % 2 for node in range(nodes)]
        form(0, 0, slots[0], 0, state_size)

        def slab_step(slab, current):
            def force(node):
                return is_last * slab_data[slab, node, :].reshape(1, state_size)

            for step in range(step_count):
                first, mid, last = 2 * step, 2 * step + 1, 2 * step + 2
                form(slab, mid, slots[mid], 0, state_size)
                slope_one = apply_op(current, slots[first]) + force(first)
                form(slab, last, slots[last], 0, state_size // 2)
                slope_two = apply_op(current + 0.5 * step_size * slope_one, slots[mid]) + force(mid)
                form(slab, last, slots[last], state_size // 2, state_size)
                slope_three = apply_op(current + 0.5 * step_size * slope_two, slots[mid]) + force(mid)
                if step == step_count - 1:
                    form(jnp.minimum(slab + 1, span - 1), 0, slots[0], 0, state_size)
                slope_four = apply_op(current + step_size * slope_three, slots[last]) + force(last)
                current = current + (step_size / 6.0) * (slope_one + 2.0 * slope_two + 2.0 * slope_three + slope_four)
            panels[pl.ds(slab, 1)] = current[None]
            return current

        lax.fori_loop(0, span, slab_step, start)

    vmem = pl.BlockSpec(memory_space=pltpu.VMEM)
    square = (state_size, state_size)
    return pl.pallas_call(
        kernel,
        out_shape=jax.ShapeDtypeStruct((span, rows, state_size), full),
        in_specs=[vmem] * 4,
        out_specs=vmem,
        scratch_shapes=[pltpu.VMEM(square, full)] * 2 + [pltpu.VMEM(square, half)] * 6,
        compiler_params=pltpu.CompilerParams(vmem_limit_bytes=60 * 1024 * 1024),
    )


def shards(initial_state, coupling, modulation, gains, forcing):
    state_size = coupling.shape[0]
    nodes = gains.shape[1]
    time_parts, col_parts = lax.axis_size("tm"), lax.axis_size("col")
    span = group_span(state_size, time_parts, col_parts)
    groups = time_parts // span
    members = span * col_parts
    cols = state_size // members
    time_index, col_index = lax.axis_index("tm"), lax.axis_index("col")
    group = time_index // span
    slab = time_index % span
    member = slab * col_parts + col_index
    teams = [[g * span + i for i in range(span)] for g in range(groups)]

    gain_row = jnp.pad(jnp.repeat(gains[0], 128), (0, state_size - nodes * 128))
    own = jnp.concatenate([forcing[0], gain_row[None]], axis=0)
    slab_data = lax.all_to_all(jnp.broadcast_to(own, (span,) + own.shape), "tm", 0, 0, axis_index_groups=teams)

    panels = panel_kernel(state_size, nodes, span, cols)(coupling, modulation, initial_state[None], slab_data)
    response = panels[:, -1, :]

    def own_cols(value):
        return lax.dynamic_slice_in_dim(value, member * cols, cols, 0)

    arrived = lax.ppermute(response[-1], "tm", [(i, (i + span) % time_parts) for i in range(time_parts)])
    begin = jnp.where(group == 1, own_cols(arrived), 0.0)
    for turn in range(1, groups - 1):
        partial = jnp.sum(panels[-1, :cols, :] * begin[:, None], axis=0)
        partial = partial + jnp.where(member == 0, 1.0, 0.0) * response[-1]
        outgoing = jnp.zeros((time_parts * col_parts, cols), full)
        outgoing = lax.dynamic_update_slice_in_dim(outgoing, partial.reshape(members, cols), ((group + 1) % groups) * members, 0)
        incoming = lax.all_to_all(outgoing, ("tm", "col"), 0, 0)
        begin = jnp.where(group == turn + 1, jnp.sum(incoming, axis=0), begin)

    partials = jnp.sum(panels[:, :cols, :] * begin[None, :, None], axis=1)
    received = lax.all_to_all(partials, "tm", 0, 0, axis_index_groups=teams)
    summed = jnp.sum(received, axis=0).reshape(col_parts, state_size // col_parts)
    slab_end = lax.psum_scatter(summed, "col", scatter_dimension=0) if col_parts != 2 else (
        lax.dynamic_index_in_dim(summed, col_index, 0, False)
        + lax.ppermute(lax.dynamic_index_in_dim(summed, 1 - col_index, 0, False), "col", [(0, 1), (1, 0)])
    )
    own_response = lax.dynamic_index_in_dim(response, slab, 0, False).reshape(col_parts, -1)
    slab_end = slab_end + lax.dynamic_index_in_dim(own_response, col_index, 0, False)
    return slab_end[None, :]


def solution(mesh):
    in_specs = (P(), P(), P(), P("tm", None), P("tm", None, None))
    out_specs = P("tm", "col")
    return jax.shard_map(shards, mesh=mesh, in_specs=in_specs, out_specs=out_specs, check_vma=False)
```

profile of v0, /device:TPU:0, one launch (start us, length us, event | category | flops | bytes accessed | tf_op | source)
XLA Modules:
  0.0 101.2 jit_solution(10051138903167005223)
XLA Ops:
  0.0 0.0 copy-start
  0.0 0.7 copy-done
  0.7 0.1 broadcast_bitcast_fusion
  0.7 0.7 copy.8
  1.5 12.7 %all_to_all.14.slab_data = f32[8,6,1024]{2,1,0:T(8,128)} all-to-all(f32[8,6,1024]{2,1,0:T(8,128)S(1)} %broadcast_in_dim.23), channel_id=1, replica_groups={{0,2,4,6,8,10,12,14},{16,18,20,22,24,26,28,30},{1,3,5,7,9,11,13,15},{17..., dimensions={0} | all-to-all | bytes 393216 | tf_op jit(solution)/shard_map/all_to_all | solution.py:125
  14.2 68.2 %shard_map.55 = f32[8,80,1024]{2,1,0:T(8,128)} custom-call(f32[1024,1024]{1,0:T(8,128)} %coupling.1, f32[1024,1024]{1,0:T(8,128)} %modulation.1, f32[1,1024]{1,0:T(1,128)} %bitcast.18, f32[8,6,1024]{2,1,0:T(8,128)} %all_to_all.14.slab_data), custom_call_target="tpu_custom_call" | custom-call | tf_op jit(solution)/shard_map/pallas_call | solution.py:127
  82.5 0.8 slice.15
  83.2 2.6 %collective-permute-start = (f32[1024]{0:T(1024)S(1)}, f32[1024]{0:T(1024)S(1)}, u32[]{:S(2)}, u32[]{:S(2)}) collective-permute-start(f32[1024]{0:T(1024)S(1)} %bitcast.19), channel_id=1, source_target_pairs={{0,16},{2,18},{4,20},{6,22},{8,24},{10,26},{12,28},{14,30},{16,0},... | collective-permute-start | bytes 12296 | tf_op jit(solution)/shard_map/ppermute | solution.py:133
  85.8 1.9 %collective-permute-done = f32[1024]{0:T(1024)S(1)} collective-permute-done((f32[1024]{0:T(1024)S(1)}, f32[1024]{0:T(1024)S(1)}, u32[]{:S(2)}, u32[]{:S(2)}) %collective-permute-start) | collective-permute-done | bytes 4128 | tf_op jit(solution)/shard_map/ppermute | solution.py:133
  87.7 0.1 broadcast_select_fusion
  87.8 1.9 %fusion = f32[8,1024]{1,0:T(8,128)S(1)} fusion(f32[8,80,1024]{2,1,0:T(8,128)} %shard_map.55, f32[64]{0:T(128)S(1)} %broadcast_select_fusion), kind=kLoop, calls=%fused_computation.1 | loop fusion | flops 1040384 | bytes 2130176 | tf_op jit(solution)/shard_map/reduce_sum | solution.py:143
  89.8 0.6 all_to_all.10
  90.4 3.3 %all-to-all-start.1 = ((f32[8,1,1024]{2,1,0:T(1,128)}), f32[8,1,1024]{2,1,0:T(1,128)S(1)}, u32[]{:S(2)}, u32[]{:S(2)}) async-start(f32[8,1,1024]{2,1,0:T(1,128)} %all_to_all.10), calls=%async_computation.1 | async-start | bytes 65536 | tf_op jit(solution)/shard_map/all_to_all | solution.py:144
  93.7 1.0 slice.16
  94.7 4.6 %all-to-all-done.1 = f32[8,1,1024]{2,1,0:T(1,128)S(1)} async-done(((f32[8,1,1024]{2,1,0:T(1,128)}), f32[8,1,1024]{2,1,0:T(1,128)S(1)}, u32[]{:S(2)}, u32[]{:S(2)}) %all-to-all-start.1) | async-done | bytes 32800 | tf_op jit(solution)/shard_map/all_to_all | solution.py:144
  99.4 0.1 collective-permute-start.1
  99.5 1.1 %collective-permute-done.1 = f32[512]{0:T(512)S(1)} collective-permute-done((f32[512]{0:T(512)S(1)}, f32[512]{0:T(512)S(1)}, u32[]{:S(2)}, u32[]{:S(2)}) %collective-permute-start.1) | collective-permute-done | bytes 2080 | tf_op jit(solution)/shard_map/ppermute | solution.py:148
  100.6 0.6 add_add_fusion
  (9 shorter events, 0.1 us)
Async XLA Ops:
  0.0 0.7 copy-start
  83.2 4.5 %collective-permute-start = (f32[1024]{0:T(1024)S(1)}, f32[1024]{0:T(1024)S(1)}, u32[]{:S(2)}, u32[]{:S(2)}) collective-permute-start(f32[1024]{0:T(1024)S(1)} %bitcast.19), channel_id=1, source_target_pairs={{0,16},{2,18},{4,20},{6,22},{8,24},{10,26},{12,28},{14,30},{16,0},... | collective-permute-start | bytes 12296 | tf_op jit(solution)/shard_map/ppermute | solution.py:133
  90.4 9.0 %all-to-all-start.1 = ((f32[8,1,1024]{2,1,0:T(1,128)}), f32[8,1,1024]{2,1,0:T(1,128)S(1)}, u32[]{:S(2)}, u32[]{:S(2)}) async-start(f32[8,1,1024]{2,1,0:T(1,128)} %all_to_all.10), calls=%async_computation.1 | async-start | bytes 65536 | tf_op jit(solution)/shard_map/all_to_all | solution.py:144
  99.4 1.2 %collective-permute-start.1 = (f32[512]{0:T(512)S(1)}, f32[512]{0:T(512)S(1)}, u32[]{:S(2)}, u32[]{:S(2)}) collective-permute-start(f32[512]{0:T(512)S(1)} %bitcast.20), channel_id=1, source_target_pairs={{0,1},{1,0},{2,3},{3,2},{4,5},{5,4},{6,7},{7,6},{8,9},{9,8},{10,11... | collective-permute-start | bytes 6152 | tf_op jit(solution)/shard_map/ppermute | solution.py:148
where the time goes:
time: 102 us; the launch traced here: 101 us
  Pallas kernels  68.2 us (67%)
  blocking collectives  12.7 us (12%)
  waiting for transfers between devices  7.65 us (8%)
  starting transfers between devices  5.99 us (6%)
  local copies, waits for them, and re-layouts  3.91 us (4%)
  other arithmetic  2.63 us (3%)
    pallas_call x1, Pallas kernels, shards(): panel_kernel(state_size, nodes, span, cols)  68.2 us
    all_to_all x1, blocking collectives, shards(): lax.all_to_all(jnp.broadcast_to(own, (span,) + own.shape), 'tm', 0, 0, ax...  12.7 us
    all_to_all x1, waiting for transfers between devices, shards(): received = lax.all_to_all(partials, 'tm', 0, 0, axis_index_groups=teams)  4.6 us
    all_to_all x1, starting transfers between devices, shards(): received = lax.all_to_all(partials, 'tm', 0, 0, axis_index_groups=teams)  3.33 us
    ppermute x1, starting transfers between devices, shards(): lax.ppermute(response[-1], 'tm', [(i, (i + span) % time_parts) for i in r...  2.59 us
  transfers between devices with their start and end apart: 3, of which 3 were waited for; matrix products, arithmetic and copies ran while one was open for 1% of the time, Pallas kernels for 0%

commit v1 on v0

--- a/solution.py
+++ b/solution.py
@@ -9,7 +9,7 @@
 half = jnp.bfloat16
 full = jnp.float32
 tile = 256
-min_cols = 64
+min_cols = 128
 spare_rows = 16
 
 

time: 102 us -> 100 us (0.980)
  Pallas kernels: 68.2 us -> 43.3 us
  waiting for transfers between devices: 7.65 us -> 23 us
  other arithmetic: 2.63 us -> 7.79 us
  starting transfers between devices: 5.99 us -> 9.89 us
  blocking collectives: 12.7 us -> 10.1 us
  local copies, waits for them, and re-layouts: 3.91 us -> 5.04 us
    pallas_call x1, Pallas kernels: 68.2 us -> 43.3 us  [shards(): panel_kernel(state_size, nodes, span, cols)]
    all_to_all x0 -> x2, waiting for transfers between devices: none -> 14.3 us  [shards(): incoming = lax.all_to_all(outgoing, ('tm', 'col'), 0, 0)]
    all_to_all x0 -> x2, starting transfers between devices: none -> 5.01 us  [shards(): incoming = lax.all_to_all(outgoing, ('tm', 'col'), 0, 0)]
    dynamic_update_slice x0 -> x2, other arithmetic: none -> 2.72 us  [shards(): lax.dynamic_update_slice_in_dim(outgoing, partial.reshape(members, cols),...]
    all_to_all x1, blocking collectives: 12.7 us -> 10.1 us  [shards(): lax.all_to_all(jnp.broadcast_to(own, (span,) + own.shape), 'tm', 0, 0, ax...]
    reduce_sum x0 -> x4, other arithmetic: none -> 2.4 us  [the longest x2 2.3 us: shards(): partial = jnp.sum(panels[-1, :cols, :] * begin[:, None], axis=0)]
    ppermute x1, waiting for transfers between devices: 1.91 us -> 3.84 us  [shards(): lax.ppermute(response[-1], 'tm', [(i, (i + span) % time_parts) for i in r...]
    all_to_all x0 -> x2, local copies, waits for them, and re-layouts: none -> 1.21 us  [shards(): incoming = lax.all_to_all(outgoing, ('tm', 'col'), 0, 0)]
  transfers between devices with their start and end apart: 3 -> 5, of which waited for: 3 -> 5; matrix products, arithmetic and copies ran while one was open for 1% -> 1% of each run, Pallas kernels for 0% -> 0%
where the time goes in v1:
time: 100 us; the launch traced here: 99.3 us
  Pallas kernels  43.3 us (43%)
  waiting for transfers between devices  23 us (23%)
  blocking collectives  10.1 us (10%)
  starting transfers between devices  9.89 us (10%)
  other arithmetic  7.79 us (8%)
  local copies, waits for them, and re-layouts  5.04 us (5%)
    pallas_call x1, Pallas kernels, shards(): panel_kernel(state_size, nodes, span, cols)  43.3 us
    all_to_all x2, waiting for transfers between devices, shards(): incoming = lax.all_to_all(outgoing, ('tm', 'col'), 0, 0)  14.3 us
    all_to_all x1, blocking collectives, shards(): lax.all_to_all(jnp.broadcast_to(own, (span,) + own.shape), 'tm', 0, 0, ax...  10.1 us
    all_to_all x2, starting transfers between devices, shards(): incoming = lax.all_to_all(outgoing, ('tm', 'col'), 0, 0)  5.01 us
    ppermute x1, waiting for transfers between devices, shards(): lax.ppermute(response[-1], 'tm', [(i, (i + span) % time_parts) for i in r...  3.84 us
    all_to_all x1, waiting for transfers between devices, shards(): received = lax.all_to_all(partials, 'tm', 0, 0, axis_index_groups=teams)  3.71 us
    all_to_all x1, starting transfers between devices, shards(): received = lax.all_to_all(partials, 'tm', 0, 0, axis_index_groups=teams)  3.25 us
    dynamic_update_slice x2, other arithmetic, shards(): lax.dynamic_update_slice_in_dim(outgoing, partial.reshape(members, cols),...  2.72 us
  transfers between devices with their start and end apart: 5, of which 5 were waited for; matrix products, arithmetic and copies ran while one was open for 1% of the time, Pallas kernels for 0%

profile of v1, /device:TPU:0, one launch (start us, length us, event | category | flops | bytes accessed | tf_op | source)
XLA Modules:
  0.0 99.3 jit_solution(9563743826136937521)
XLA Ops:
  0.0 0.0 copy-start
  0.0 0.7 copy-done
  0.7 0.1 broadcast_bitcast_fusion
  0.7 0.7 copy.10
  1.5 10.1 %all_to_all.29.slab_data = f32[4,6,1024]{2,1,0:T(8,128)} all-to-all(f32[4,6,1024]{2,1,0:T(8,128)S(1)} %broadcast_in_dim.25), channel_id=1, replica_groups={{0,2,4,6},{8,10,12,14},{16,18,20,22},{24,26,28,30},{1,3,5,7},{9,11,13,1..., dimensions={0} | all-to-all | bytes 196608 | tf_op jit(solution)/shard_map/all_to_all | solution.py:125
  11.6 43.3 %shard_map.55 = f32[4,144,1024]{2,1,0:T(8,128)} custom-call(f32[1024,1024]{1,0:T(8,128)} %coupling.1, f32[1024,1024]{1,0:T(8,128)} %modulation.1, f32[1,1024]{1,0:T(1,128)} %bitcast.37, f32[4,6,1024]{2,1,0:T(8,128)} %all_to_all.29.slab_data), custom_call_target="tpu_custom_call" | custom-call | tf_op jit(solution)/shard_map/pallas_call | solution.py:127
  54.9 0.8 slice.23
  55.7 1.6 %collective-permute-start = (f32[1024]{0:T(1024)S(1)}, f32[1024]{0:T(1024)S(1)}, u32[]{:S(2)}, u32[]{:S(2)}) collective-permute-start(f32[1024]{0:T(1024)S(1)} %bitcast.38), channel_id=1, source_target_pairs={{0,8},{2,10},{4,12},{6,14},{8,16},{10,18},{12,20},{14,22},{16,24},... | collective-permute-start | bytes 12296 | tf_op jit(solution)/shard_map/ppermute | solution.py:133
  57.3 3.8 %collective-permute-done = f32[1024]{0:T(1024)S(1)} collective-permute-done((f32[1024]{0:T(1024)S(1)}, f32[1024]{0:T(1024)S(1)}, u32[]{:S(2)}, u32[]{:S(2)}) %collective-permute-start) | collective-permute-done | bytes 4128 | tf_op jit(solution)/shard_map/ppermute | solution.py:133
  61.1 0.1 broadcast_select_fusion
  61.2 1.1 %multiply_reduce_fusion.1 = f32[1024]{0:T(1024)S(1)} fusion(f32[4,144,1024]{2,1,0:T(8,128)} %shard_map.55, f32[128]{0:T(128)S(1)} %broadcast_select_fusion), kind=kLoop, calls=%fused_computation.4 | loop fusion | flops 261120 | bytes 528896 | tf_op jit(solution)/shard_map/reduce_sum | solution.py:136
  62.3 0.6 all_to_all.20.clone
  62.9 1.4 %fusion.1 = f32[32,1,128]{2,1,0:T(1,128)} fusion(f32[32,1,128]{2,1,0:T(1,128)} %all_to_all.20.clone, s32[]{:T(128)S(6)} %select_n.72, f32[8,1,128]{2,1,0:T(1,128)S(1)} %bitcast.33, f32[]{:T(128)S(6)} %select_n.70, f32[4,144,1024]{2,1,0:T(8,128)} %shard_map.55), kind=kLoop, calls=%fused_computation.9 | loop fusion | flops 2048 | bytes 12296 | tf_op jit(solution)/shard_map/dynamic_update_slice | solution.py:139
  64.3 2.5 %all-to-all-start.1 = ((f32[32,1,128]{2,1,0:T(1,128)}), f32[32,1,128]{2,1,0:T(1,128)S(1)}, u32[]{:S(2)}, u32[]{:S(2)}) async-start(f32[32,1,128]{2,1,0:T(1,128)} %fusion.1), calls=%async_computation.1 | async-start | bytes 32768 | tf_op jit(solution)/shard_map/all_to_all | solution.py:140
  66.8 7.2 %all-to-all-done.1 = f32[32,1,128]{2,1,0:T(1,128)S(1)} async-done(((f32[32,1,128]{2,1,0:T(1,128)}), f32[32,1,128]{2,1,0:T(1,128)S(1)}, u32[]{:S(2)}, u32[]{:S(2)}) %all-to-all-start.1) | async-done | bytes 16416 | tf_op jit(solution)/shard_map/all_to_all | solution.py:140
  74.0 0.1 reduce_sum.60
  74.1 0.1 broadcast_select_fusion.1
  74.1 1.1 %multiply_reduce_fusion = f32[1024]{0:T(1024)S(1)} fusion(f32[4,144,1024]{2,1,0:T(8,128)} %shard_map.55, f32[128]{0:T(128)S(1)} %broadcast_select_fusion.1), kind=kLoop, calls=%fused_computation.3 | loop fusion | flops 261120 | bytes 528896 | tf_op jit(solution)/shard_map/reduce_sum | solution.py:136
  75.3 0.6 all_to_all.20
  75.9 1.4 %fusion.2 = f32[32,1,128]{2,1,0:T(1,128)} fusion(f32[32,1,128]{2,1,0:T(1,128)} %all_to_all.20, s32[]{:T(128)S(6)} %select_n.72, f32[8,1,128]{2,1,0:T(1,128)S(1)} %bitcast.32, f32[]{:T(128)S(6)} %select_n.70, f32[4,144,1024]{2,1,0:T(8,128)} %shard_map.55), kind=kLoop, calls=%fused_computation.10 | loop fusion | flops 2048 | bytes 12296 | tf_op jit(solution)/shard_map/dynamic_update_slice | solution.py:139
  77.2 2.5 %all-to-all-start.2 = ((f32[32,1,128]{2,1,0:T(1,128)}), f32[32,1,128]{2,1,0:T(1,128)S(1)}, u32[]{:S(2)}, u32[]{:S(2)}) async-start(f32[32,1,128]{2,1,0:T(1,128)} %fusion.2), calls=%async_computation.2 | async-start | bytes 32768 | tf_op jit(solution)/shard_map/all_to_all | solution.py:140
  79.7 7.2 %all-to-all-done.2 = f32[32,1,128]{2,1,0:T(1,128)S(1)} async-done(((f32[32,1,128]{2,1,0:T(1,128)}), f32[32,1,128]{2,1,0:T(1,128)S(1)}, u32[]{:S(2)}, u32[]{:S(2)}) %all-to-all-start.2) | async-done | bytes 16416 | tf_op jit(solution)/shard_map/all_to_all | solution.py:140
  86.9 0.1 reduce_sum.63
  87.0 1.9 %fusion = f32[4,1024]{1,0:T(4,128)S(1)} fusion(f32[4,144,1024]{2,1,0:T(8,128)} %shard_map.55, f32[128]{0:T(128)S(1)} %broadcast_select_fusion.2), kind=kLoop, calls=%fused_computation.1 | loop fusion | flops 1044480 | bytes 2114048 | tf_op jit(solution)/shard_map/reduce_sum | solution.py:143
  88.9 0.6 all_to_all.23
  89.5 3.2 %all-to-all-start.3 = ((f32[4,1,1024]{2,1,0:T(1,128)}), f32[4,1,1024]{2,1,0:T(1,128)S(1)}, u32[]{:S(2)}, u32[]{:S(2)}) async-start(f32[4,1,1024]{2,1,0:T(1,128)} %all_to_all.23), calls=%async_computation.3 | async-start | bytes 32768 | tf_op jit(solution)/shard_map/all_to_all | solution.py:144
  92.7 0.9 slice.24
  93.7 3.7 %all-to-all-done.3 = f32[4,1,1024]{2,1,0:T(1,128)S(1)} async-done(((f32[4,1,1024]{2,1,0:T(1,128)}), f32[4,1,1024]{2,1,0:T(1,128)S(1)}, u32[]{:S(2)}, u32[]{:S(2)}) %all-to-all-start.3) | async-done | bytes 16416 | tf_op jit(solution)/shard_map/all_to_all | solution.py:144
  97.5 0.1 collective-permute-start.1
  97.6 1.1 %collective-permute-done.1 = f32[512]{0:T(512)S(1)} collective-permute-done((f32[512]{0:T(512)S(1)}, f32[512]{0:T(512)S(1)}, u32[]{:S(2)}, u32[]{:S(2)}) %collective-permute-start.1) | collective-permute-done | bytes 2080 | tf_op jit(solution)/shard_map/ppermute | solution.py:148
  98.7 0.6 add_add_fusion
  (10 shorter events, 0.1 us)
Async XLA Ops:
  0.0 0.7 copy-start
  55.7 5.4 %collective-permute-start = (f32[1024]{0:T(1024)S(1)}, f32[1024]{0:T(1024)S(1)}, u32[]{:S(2)}, u32[]{:S(2)}) collective-permute-start(f32[1024]{0:T(1024)S(1)} %bitcast.38), channel_id=1, source_target_pairs={{0,8},{2,10},{4,12},{6,14},{8,16},{10,18},{12,20},{14,22},{16,24},... | collective-permute-start | bytes 12296 | tf_op jit(solution)/shard_map/ppermute | solution.py:133
  64.3 9.7 %all-to-all-start.1 = ((f32[32,1,128]{2,1,0:T(1,128)}), f32[32,1,128]{2,1,0:T(1,128)S(1)}, u32[]{:S(2)}, u32[]{:S(2)}) async-start(f32[32,1,128]{2,1,0:T(1,128)} %fusion.1), calls=%async_computation.1 | async-start | bytes 32768 | tf_op jit(solution)/shard_map/all_to_all | solution.py:140
  77.2 9.7 %all-to-all-start.2 = ((f32[32,1,128]{2,1,0:T(1,128)}), f32[32,1,128]{2,1,0:T(1,128)S(1)}, u32[]{:S(2)}, u32[]{:S(2)}) async-start(f32[32,1,128]{2,1,0:T(1,128)} %fusion.2), calls=%async_computation.2 | async-start | bytes 32768 | tf_op jit(solution)/shard_map/all_to_all | solution.py:140
  89.5 7.9 %all-to-all-start.3 = ((f32[4,1,1024]{2,1,0:T(1,128)}), f32[4,1,1024]{2,1,0:T(1,128)S(1)}, u32[]{:S(2)}, u32[]{:S(2)}) async-start(f32[4,1,1024]{2,1,0:T(1,128)} %all_to_all.23), calls=%async_computation.3 | async-start | bytes 32768 | tf_op jit(solution)/shard_map/all_to_all | solution.py:144
  97.5 1.2 %collective-permute-start.1 = (f32[512]{0:T(512)S(1)}, f32[512]{0:T(512)S(1)}, u32[]{:S(2)}, u32[]{:S(2)}) collective-permute-start(f32[512]{0:T(512)S(1)} %bitcast.39), channel_id=1, source_target_pairs={{0,1},{1,0},{2,3},{3,2},{4,5},{5,4},{6,7},{7,6},{8,9},{9,8},{10,11... | collective-permute-start | bytes 6152 | tf_op jit(solution)/shard_map/ppermute | solution.py:148

commit v2 on v1

--- a/solution.py
+++ b/solution.py
@@ -30,7 +30,7 @@
     step_count = (nodes - 1) // 2
     blocks = state_size // tile
 
-    def kernel(coupling, modulation, initial, slab_data, panels, base, vary, *splits):
+    def kernel(coupling, modulation, initial, slab_data, panels, responses, base, vary, *splits):
         highs, lows = splits[:3], splits[3:]
 
         def build(source, target):
@@ -89,7 +89,8 @@
                     form(jnp.minimum(slab + 1, span - 1), 0, slots[0], 0, state_size)
                 slope_four = apply_op(current + step_size * slope_three, slots[last]) + force(last)
                 current = current + (step_size / 6.0) * (slope_one + 2.0 * slope_two + 2.0 * slope_three + slope_four)
-            panels[pl.ds(slab, 1)] = current[None]
+            panels[pl.ds(slab, 1)] = current[None, :cols]
+            responses[pl.ds(slab, 1)] = current[None, rows - 1:rows]
             return current
 
         lax.fori_loop(0, span, slab_step, start)
@@ -98,12 +99,61 @@
     square = (state_size, state_size)
     return pl.pallas_call(
         kernel,
-        out_shape=jax.ShapeDtypeStruct((span, rows, state_size), full),
+        out_shape=[jax.ShapeDtypeStruct((span, count, state_size), full) for count in (cols, 1)],
         in_specs=[vmem] * 4,
-        out_specs=vmem,
+        out_specs=[vmem] * 2,
         scratch_shapes=[pltpu.VMEM(square, full)] * 2 + [pltpu.VMEM(square, half)] * 6,
         compiler_params=pltpu.CompilerParams(vmem_limit_bytes=60 * 1024 * 1024),
     )
+
+
+def weighted_rows(weights, panel):
+    high, low = split(jnp.broadcast_to(weights, (16, weights.shape[1])))
+    panel_high, panel_low = split(panel)
+    total = jnp.dot(high, panel_high, preferred_element_type=full)
+    total = total + jnp.dot(low, panel_high, preferred_element_type=full)
+    return (total + jnp.dot(high, panel_low, preferred_element_type=full))[:1]
+
+
+def hop_blocks(panels, responses, begin, share, members, copies):
+    span, cols, state_size = panels.shape
+
+    def kernel(weights, factor, panel, response, blocks):
+        total = weighted_rows(weights[...], panel[0]) + factor[...] * response[0]
+        for copy in range(copies):
+            for member in range(members):
+                blocks[copy * members + member] = total[:, member * cols:(member + 1) * cols]
+
+    return pl.pallas_call(
+        kernel,
+        grid=(1,),
+        out_shape=jax.ShapeDtypeStruct((copies * members, 1, cols), full),
+        in_specs=[
+            pl.BlockSpec((1, cols), lambda i: (0, 0)),
+            pl.BlockSpec((1, state_size), lambda i: (0, 0)),
+            pl.BlockSpec((1, cols, state_size), lambda i: (span - 1, 0, 0)),
+            pl.BlockSpec((1, 1, state_size), lambda i: (span - 1, 0, 0)),
+        ],
+        out_specs=pl.BlockSpec((copies * members, 1, cols), lambda i: (0, 0, 0)),
+    )(begin, share, panels, responses)
+
+
+def slab_shares(panels, begin):
+    span, cols, state_size = panels.shape
+
+    def kernel(weights, panel, shares):
+        shares[0] = weighted_rows(weights[...], panel[0])
+
+    return pl.pallas_call(
+        kernel,
+        grid=(span,),
+        out_shape=jax.ShapeDtypeStruct((span, 1, state_size), full),
+        in_specs=[
+            pl.BlockSpec((1, cols), lambda i: (0, 0)),
+            pl.BlockSpec((1, cols, state_size), lambda i: (i, 0, 0)),
+        ],
+        out_specs=pl.BlockSpec((1, 1, state_size), lambda i: (i, 0, 0)),
+    )(begin, panels)
 
 
 def shards(initial_state, coupling, modulation, gains, forcing):
@@ -124,30 +174,30 @@
     own = jnp.concatenate([forcing[0], gain_row[None]], axis=0)
     slab_data = lax.all_to_all(jnp.broadcast_to(own, (span,) + own.shape), "tm", 0, 0, axis_index_groups=teams)
 
-    panels = panel_kernel(state_size, nodes, span, cols)(coupling, modulation, initial_state[None], slab_data)
-    response = panels[:, -1, :]
-
-    def own_cols(value):
-        return lax.dynamic_slice_in_dim(value, member * cols, cols, 0)
-
-    arrived = lax.ppermute(response[-1], "tm", [(i, (i + span) % time_parts) for i in range(time_parts)])
-    begin = jnp.where(group == 1, own_cols(arrived), 0.0)
+    panels, responses = panel_kernel(state_size, nodes, span, cols)(coupling, modulation, initial_state[None], slab_data)
+
+    if groups % 2 == 0:
+        first_hop = [(i, i + span if i // span % 2 == 0 else i - span) for i in range(time_parts)]
+    else:
+        first_hop = [(i, (i + span) % time_parts) for i in range(time_parts)]
+    arrived = lax.ppermute(responses[-1], "tm", first_hop)
+    begin = lax.dynamic_slice_in_dim(arrived, member * cols, cols, 1)
+    begin = jnp.where(group == 1, begin, 0.0)
+    share = jnp.full((1, state_size), jnp.where(member == 0, 1.0, 0.0))
+    source_group = jnp.arange(time_parts * col_parts).reshape(-1, 1, 1) // members
     for turn in range(1, groups - 1):
-        partial = jnp.sum(panels[-1, :cols, :] * begin[:, None], axis=0)
-        partial = partial + jnp.where(member == 0, 1.0, 0.0) * response[-1]
-        outgoing = jnp.zeros((time_parts * col_parts, cols), full)
-        outgoing = lax.dynamic_update_slice_in_dim(outgoing, partial.reshape(members, cols), ((group + 1) % groups) * members, 0)
-        incoming = lax.all_to_all(outgoing, ("tm", "col"), 0, 0)
-        begin = jnp.where(group == turn + 1, jnp.sum(incoming, axis=0), begin)
-
-    partials = jnp.sum(panels[:, :cols, :] * begin[None, :, None], axis=1)
-    received = lax.all_to_all(partials, "tm", 0, 0, axis_index_groups=teams)
+        outgoing = hop_blocks(panels, responses, begin, share, members, groups)
+        incoming = lax.all_to_all(outgoing, ("tm", "col"), 0, 0, tiled=True)
+        summed = jnp.sum(jnp.where(source_group == group - 1, incoming, 0.0), axis=0)
+        begin = jnp.where(group == turn + 1, summed, begin)
+
+    received = lax.all_to_all(slab_shares(panels, begin), "tm", 0, 0, axis_index_groups=teams, tiled=True)
     summed = jnp.sum(received, axis=0).reshape(col_parts, state_size // col_parts)
     slab_end = lax.psum_scatter(summed, "col", scatter_dimension=0) if col_parts != 2 else (
         lax.dynamic_index_in_dim(summed, col_index, 0, False)
         + lax.ppermute(lax.dynamic_index_in_dim(summed, 1 - col_index, 0, False), "col", [(0, 1), (1, 0)])
     )
-    own_response = lax.dynamic_index_in_dim(response, slab, 0, False).reshape(col_parts, -1)
+    own_response = lax.dynamic_index_in_dim(responses, slab, 0, False).reshape(col_parts, -1)
     slab_end = slab_end + lax.dynamic_index_in_dim(own_response, col_index, 0, False)
     return slab_end[None, :]
 

time: 100 us -> 103 us (1.030)
  blocking collectives: 10.1 us -> 0 us
  Pallas kernels: 43.3 us -> 50.8 us
  starting transfers between devices: 9.89 us -> 17 us
  other arithmetic: 7.79 us -> 3.06 us
  waiting for transfers between devices: 23 us -> 27.2 us
    all_to_all x1 -> x0, blocking collectives: 10.1 us -> none  [shards(): lax.all_to_all(jnp.broadcast_to(own, (span,) + own.shape), 'tm', 0, 0, ax...]
    pallas_call x0 -> x3, Pallas kernels: none -> 7.57 us  [the longest x2 3.79 us: hop_blocks(): pl.pallas_call(kernel, grid=(1,), out_shape=jax.ShapeDtypeStruct((copies...]
    all_to_all x3 -> x4, starting transfers between devices: 8.25 us -> 15.3 us  [the longest x2 6.87 us: shards(): incoming = lax.all_to_all(outgoing, ('tm', 'col'), 0, 0, tiled=True)]
    all_to_all x3 -> x4, waiting for transfers between devices: 18 us -> 24 us  [the longest x2 14.3 us: shards(): incoming = lax.all_to_all(outgoing, ('tm', 'col'), 0, 0, tiled=True)]
    reduce_sum x5 -> x2, other arithmetic: 4.29 us -> 0.23 us  [shards(): jnp.sum(jnp.where(source_group == group - 1, incoming, 0.0), axis=0)]
    dynamic_update_slice x2 -> x0, other arithmetic: 2.72 us -> none  [shards(): lax.dynamic_update_slice_in_dim(outgoing, partial.reshape(members, cols),...]
    select_n x3, other arithmetic: 0.16 us -> 2.21 us  [the longest x2 1.69 us: shards(): begin = jnp.where(group == turn + 1, summed, begin)]
    all_to_all x3 -> x0, local copies, waits for them, and re-layouts: 1.82 us -> none  [the longest x2 1.21 us: shards(): incoming = lax.all_to_all(outgoing, ('tm', 'col'), 0, 0)]
  transfers between devices with their start and end apart: 5 -> 6, of which waited for: 5 -> 6; matrix products, arithmetic and copies ran while one was open for 1% -> 0% of each run, Pallas kernels for 0% -> 0%
where the time goes in v2:
time: 103 us; the launch traced here: 102 us
  Pallas kernels  50.8 us (49%)
  waiting for transfers between devices  27.2 us (26%)
  starting transfers between devices  17 us (17%)
  local copies, waits for them, and re-layouts  4.09 us (4%)
  other arithmetic  3.06 us (3%)
    pallas_call x1, Pallas kernels, shards(): panel_kernel(state_size, nodes, span, cols)  43.2 us
    all_to_all x2, waiting for transfers between devices, shards(): incoming = lax.all_to_all(outgoing, ('tm', 'col'), 0, 0, tiled=True)  14.3 us
    all_to_all x2, starting transfers between devices, shards(): incoming = lax.all_to_all(outgoing, ('tm', 'col'), 0, 0, tiled=True)  6.87 us
    all_to_all x1, starting transfers between devices, shards(): lax.all_to_all(jnp.broadcast_to(own, (span,) + own.shape), 'tm', 0, 0, ax...  5.19 us
    all_to_all x1, waiting for transfers between devices, shards(): lax.all_to_all(jnp.broadcast_to(own, (span,) + own.shape), 'tm', 0, 0, ax...  5.02 us
    all_to_all x1, waiting for transfers between devices, shards(): lax.all_to_all(slab_shares(panels, begin), 'tm', 0, 0, axis_index_groups=...  4.67 us
    pallas_call x2, Pallas kernels, hop_blocks(): pl.pallas_call(kernel, grid=(1,), out_shape=jax.ShapeDtypeStruct((copies...  3.79 us
    pallas_call x1, Pallas kernels, slab_shares(): pl.pallas_call(kernel, grid=(span,), out_shape=jax.ShapeDtypeStruct((span...  3.78 us
  transfers between devices with their start and end apart: 6, of which 6 were waited for; matrix products, arithmetic and copies ran while one was open for 0% of the time, Pallas kernels for 0%

profile of v2, /device:TPU:0, one launch (start us, length us, event | category | flops | bytes accessed | tf_op | source)
XLA Modules:
  0.0 102.2 jit_solution(15534372993518064809)
XLA Ops:
  0.0 0.0 copy-start
  0.0 0.7 copy-done
  0.7 0.1 broadcast_bitcast_fusion
  0.7 0.7 copy.8
  1.5 0.7 broadcast_in_dim.42
  2.1 5.2 %all-to-all-start = ((f32[4,6,1024]{2,1,0:T(8,128)}), f32[4,6,1024]{2,1,0:T(8,128)S(1)}, u32[]{:S(2)}, u32[]{:S(2)}) async-start(f32[4,6,1024]{2,1,0:T(8,128)} %broadcast_in_dim.42), calls=%async_computation | async-start | bytes 262144 | tf_op jit(solution)/shard_map/all_to_all | solution.py:175
  7.3 5.0 %all-to-all-done.slab_data = f32[4,6,1024]{2,1,0:T(8,128)S(1)} async-done(((f32[4,6,1024]{2,1,0:T(8,128)}), f32[4,6,1024]{2,1,0:T(8,128)S(1)}, u32[]{:S(2)}, u32[]{:S(2)}) %all-to-all-start) | async-done | bytes 98336 | tf_op jit(solution)/shard_map/all_to_all | solution.py:175
  12.4 0.0 copy-start.1
  12.4 0.6 copy-done.1
  13.0 43.2 %shard_map.55 = (f32[4,128,1024]{2,1,0:T(8,128)}, f32[4,1,1024]{2,1,0:T(1,128)}) custom-call(f32[1024,1024]{1,0:T(8,128)} %coupling.1, f32[1024,1024]{1,0:T(8,128)} %modulation.1, f32[1,1024]{1,0:T(1,128)} %bitcast.23, f32[4,6,1024]{2,1,0:T(8,128)} %copy-done.1), custom_call_target="tpu_custom_call" | custom-call | tf_op jit(solution)/shard_map/pallas_call | solution.py:177
  56.2 0.7 slice_bitcast_fusion
  56.9 1.6 %collective-permute-start = (f32[1,1024]{1,0:T(1,128)S(1)}, f32[1,1024]{1,0:T(1,128)S(1)}, u32[]{:S(2)}, u32[]{:S(2)}) collective-permute-start(f32[1,1024]{1,0:T(1,128)S(1)} %get-tuple-element.9), channel_id=1, source_target_pairs={{0,8},{2,10},{4,12},{6,14},{8,0},{10,2},{12,4},{14,6},{16,24},{18,... | collective-permute-start | bytes 12296 | tf_op jit(solution)/shard_map/ppermute | solution.py:183
  58.6 2.0 %collective-permute-done = f32[1,1024]{1,0:T(1,128)S(1)} collective-permute-done((f32[1,1024]{1,0:T(1,128)S(1)}, f32[1,1024]{1,0:T(1,128)S(1)}, u32[]{:S(2)}, u32[]{:S(2)}) %collective-permute-start) | collective-permute-done | bytes 4128 | tf_op jit(solution)/shard_map/ppermute | solution.py:183
  60.6 0.5 broadcast_select_fusion.2.weights
  61.1 0.6 broadcast_in_dim.44.factor
  61.7 1.9 %shard_map.56 = f32[32,1,128]{2,1,0:T(1,128)} custom-call(f32[1,128]{1,0:T(1,128)} %broadcast_select_fusion.2.weights, f32[1,1024]{1,0:T(1,128)} %broadcast_in_dim.44.factor, f32[4,128,1024]{2,1,0:T(8,128)} %get-tuple-element.8.panel, f32[4,1,1024]{2,1,0:T(1,128)} %get-tuple-element.7.response), custom_call_target="tpu_custom_call" | custom-call | tf_op jit(solution)/shard_map/pallas_call | solution.py:127
  63.6 4.3 %all-to-all-start.1 = ((f32[32,1,128]{2,1,0:T(1,128)}), f32[32,1,128]{2,1,0:T(1,128)S(1)}, u32[]{:S(2)}, u32[]{:S(2)}) async-start(f32[32,1,128]{2,1,0:T(1,128)} %shard_map.56), calls=%async_computation.1 | async-start | bytes 32768 | tf_op jit(solution)/shard_map/all_to_all | solution.py:190
  67.9 7.2 %all-to-all-done.1 = f32[32,1,128]{2,1,0:T(1,128)S(1)} async-done(((f32[32,1,128]{2,1,0:T(1,128)}), f32[32,1,128]{2,1,0:T(1,128)S(1)}, u32[]{:S(2)}, u32[]{:S(2)}) %all-to-all-start.1) | async-done | bytes 16416 | tf_op jit(solution)/shard_map/all_to_all | solution.py:190
  75.1 0.1 fusion
  75.2 0.5 broadcast_select_fusion.3.weights
  75.7 1.9 %shard_map.57 = f32[32,1,128]{2,1,0:T(1,128)} custom-call(f32[1,128]{1,0:T(1,128)} %broadcast_select_fusion.3.weights, f32[1,1024]{1,0:T(1,128)} %broadcast_in_dim.44.factor, f32[4,128,1024]{2,1,0:T(8,128)} %get-tuple-element.8.panel, f32[4,1,1024]{2,1,0:T(1,128)} %get-tuple-element.7.response), custom_call_target="tpu_custom_call" | custom-call | tf_op jit(solution)/shard_map/pallas_call | solution.py:127
  77.6 2.5 %all-to-all-start.2 = ((f32[32,1,128]{2,1,0:T(1,128)}), f32[32,1,128]{2,1,0:T(1,128)S(1)}, u32[]{:S(2)}, u32[]{:S(2)}) async-start(f32[32,1,128]{2,1,0:T(1,128)} %shard_map.57), calls=%async_computation.2 | async-start | bytes 32768 | tf_op jit(solution)/shard_map/all_to_all | solution.py:190
  80.2 7.2 %all-to-all-done.2 = f32[32,1,128]{2,1,0:T(1,128)S(1)} async-done(((f32[32,1,128]{2,1,0:T(1,128)}), f32[32,1,128]{2,1,0:T(1,128)S(1)}, u32[]{:S(2)}, u32[]{:S(2)}) %all-to-all-start.2) | async-done | bytes 16416 | tf_op jit(solution)/shard_map/all_to_all | solution.py:190
  87.4 0.1 fusion.1
  87.5 1.2 %broadcast_select_fusion.4.weights = f32[1,128]{1,0:T(1,128)} fusion(f32[1,128]{1,0:T(1,128)} %broadcast_select_fusion.3.weights, pred[]{:T(512)S(6)} %eq.27, f32[128]{0:T(128)S(1)} %fusion.1), kind=kLoop, calls=%fused_computation.20 | loop fusion | flops 128 | bytes 1537 | tf_op jit(solution)/shard_map/jit(_where)/select_n | solution.py:192
  88.7 3.8 %shard_map.58 = f32[4,1,1024]{2,1,0:T(1,128)} custom-call(f32[1,128]{1,0:T(1,128)} %broadcast_select_fusion.4.weights, f32[4,128,1024]{2,1,0:T(8,128)} %get-tuple-element.8.panel), custom_call_target="tpu_custom_call" | custom-call | tf_op jit(solution)/shard_map/pallas_call | solution.py:147
  92.4 3.2 %all-to-all-start.3 = ((f32[4,1,1024]{2,1,0:T(1,128)}), f32[4,1,1024]{2,1,0:T(1,128)S(1)}, u32[]{:S(2)}, u32[]{:S(2)}) async-start(f32[4,1,1024]{2,1,0:T(1,128)} %shard_map.58), calls=%async_computation.3 | async-start | bytes 32768 | tf_op jit(solution)/shard_map/all_to_all | solution.py:194
  95.7 4.7 %all-to-all-done.3 = f32[4,1,1024]{2,1,0:T(1,128)S(1)} async-done(((f32[4,1,1024]{2,1,0:T(1,128)}), f32[4,1,1024]{2,1,0:T(1,128)S(1)}, u32[]{:S(2)}, u32[]{:S(2)}) %all-to-all-start.3) | async-done | bytes 16416 | tf_op jit(solution)/shard_map/all_to_all | solution.py:194
  100.4 0.1 collective-permute-start.1
  100.5 1.1 %collective-permute-done.1 = f32[512]{0:T(512)S(1)} collective-permute-done((f32[512]{0:T(512)S(1)}, f32[512]{0:T(512)S(1)}, u32[]{:S(2)}, u32[]{:S(2)}) %collective-permute-start.1) | collective-permute-done | bytes 2080 | tf_op jit(solution)/shard_map/ppermute | solution.py:198
  101.7 0.6 add_add_fusion
  (8 shorter events, 0.1 us)
Async XLA Ops:
  0.0 0.7 copy-start
  2.1 10.2 %all-to-all-start = ((f32[4,6,1024]{2,1,0:T(8,128)}), f32[4,6,1024]{2,1,0:T(8,128)S(1)}, u32[]{:S(2)}, u32[]{:S(2)}) async-start(f32[4,6,1024]{2,1,0:T(8,128)} %broadcast_in_dim.42), calls=%async_computation | async-start | bytes 262144 | tf_op jit(solution)/shard_map/all_to_all | solution.py:175
  12.4 0.6 copy-start.1
  56.9 3.7 %collective-permute-start = (f32[1,1024]{1,0:T(1,128)S(1)}, f32[1,1024]{1,0:T(1,128)S(1)}, u32[]{:S(2)}, u32[]{:S(2)}) collective-permute-start(f32[1,1024]{1,0:T(1,128)S(1)} %get-tuple-element.9), channel_id=1, source_target_pairs={{0,8},{2,10},{4,12},{6,14},{8,0},{10,2},{12,4},{14,6},{16,24},{18,... | collective-permute-start | bytes 12296 | tf_op jit(solution)/shard_map/ppermute | solution.py:183
  63.6 11.5 %all-to-all-start.1 = ((f32[32,1,128]{2,1,0:T(1,128)}), f32[32,1,128]{2,1,0:T(1,128)S(1)}, u32[]{:S(2)}, u32[]{:S(2)}) async-start(f32[32,1,128]{2,1,0:T(1,128)} %shard_map.56), calls=%async_computation.1 | async-start | bytes 32768 | tf_op jit(solution)/shard_map/all_to_all | solution.py:190
  77.6 9.7 %all-to-all-start.2 = ((f32[32,1,128]{2,1,0:T(1,128)}), f32[32,1,128]{2,1,0:T(1,128)S(1)}, u32[]{:S(2)}, u32[]{:S(2)}) async-start(f32[32,1,128]{2,1,0:T(1,128)} %shard_map.57), calls=%async_computation.2 | async-start | bytes 32768 | tf_op jit(solution)/shard_map/all_to_all | solution.py:190
  92.4 7.9 %all-to-all-start.3 = ((f32[4,1,1024]{2,1,0:T(1,128)}), f32[4,1,1024]{2,1,0:T(1,128)S(1)}, u32[]{:S(2)}, u32[]{:S(2)}) async-start(f32[4,1,1024]{2,1,0:T(1,128)} %shard_map.58), calls=%async_computation.3 | async-start | bytes 32768 | tf_op jit(solution)/shard_map/all_to_all | solution.py:194
  100.4 1.2 %collective-permute-start.1 = (f32[512]{0:T(512)S(1)}, f32[512]{0:T(512)S(1)}, u32[]{:S(2)}, u32[]{:S(2)}) collective-permute-start(f32[512]{0:T(512)S(1)} %bitcast.24), channel_id=1, source_target_pairs={{0,1},{1,0},{2,3},{3,2},{4,5},{5,4},{6,7},{7,6},{8,9},{9,8},{10,11... | collective-permute-start | bytes 6152 | tf_op jit(solution)/shard_map/ppermute | solution.py:198

commit v3 on v1

--- a/solution.py
+++ b/solution.py
@@ -30,7 +30,7 @@
     step_count = (nodes - 1) // 2
     blocks = state_size // tile
 
-    def kernel(coupling, modulation, initial, slab_data, panels, base, vary, *splits):
+    def kernel(coupling, modulation, initial, slab_data, panels, responses, base, vary, *splits):
         highs, lows = splits[:3], splits[3:]
 
         def build(source, target):
@@ -89,7 +89,8 @@
                     form(jnp.minimum(slab + 1, span - 1), 0, slots[0], 0, state_size)
                 slope_four = apply_op(current + step_size * slope_three, slots[last]) + force(last)
                 current = current + (step_size / 6.0) * (slope_one + 2.0 * slope_two + 2.0 * slope_three + slope_four)
-            panels[pl.ds(slab, 1)] = current[None]
+            panels[pl.ds(slab, 1)] = current[None, :cols]
+            responses[pl.ds(slab, 1)] = current[None, rows - 1:rows]
             return current
 
         lax.fori_loop(0, span, slab_step, start)
@@ -98,12 +99,27 @@
     square = (state_size, state_size)
     return pl.pallas_call(
         kernel,
-        out_shape=jax.ShapeDtypeStruct((span, rows, state_size), full),
+        out_shape=[jax.ShapeDtypeStruct((span, count, state_size), full) for count in (cols, 1)],
         in_specs=[vmem] * 4,
-        out_specs=vmem,
+        out_specs=[vmem] * 2,
         scratch_shapes=[pltpu.VMEM(square, full)] * 2 + [pltpu.VMEM(square, half)] * 6,
         compiler_params=pltpu.CompilerParams(vmem_limit_bytes=60 * 1024 * 1024),
     )
+
+
+def team_gather(value, span, teams):
+    count = value.shape[0]
+    if span & (span - 1):
+        copies = jnp.broadcast_to(value, (span,) + value.shape)
+        return lax.all_to_all(copies, "tm", 0, 0, axis_index_groups=teams).reshape((span * count,) + value.shape[1:])
+    place = lax.axis_index("tm") % span
+    step = 1
+    while step < span:
+        other = lax.ppermute(value, "tm", [(i, i ^ step) for i in range(lax.axis_size("tm"))])
+        is_upper = (place // step) % 2 == 1
+        value = jnp.concatenate([jnp.where(is_upper, other, value), jnp.where(is_upper, value, other)], axis=0)
+        step *= 2
+    return value
 
 
 def shards(initial_state, coupling, modulation, gains, forcing):
@@ -122,32 +138,34 @@
 
     gain_row = jnp.pad(jnp.repeat(gains[0], 128), (0, state_size - nodes * 128))
     own = jnp.concatenate([forcing[0], gain_row[None]], axis=0)
-    slab_data = lax.all_to_all(jnp.broadcast_to(own, (span,) + own.shape), "tm", 0, 0, axis_index_groups=teams)
+    slab_data = team_gather(own[None], span, teams)
 
-    panels = panel_kernel(state_size, nodes, span, cols)(coupling, modulation, initial_state[None], slab_data)
-    response = panels[:, -1, :]
+    panels, responses = panel_kernel(state_size, nodes, span, cols)(coupling, modulation, initial_state[None], slab_data)
 
-    def own_cols(value):
-        return lax.dynamic_slice_in_dim(value, member * cols, cols, 0)
+    if groups % 2 == 0:
+        first_hop = [(i, i + span if i // span % 2 == 0 else i - span) for i in range(time_parts)]
+    else:
+        first_hop = [(i, (i + span) % time_parts) for i in range(time_parts)]
+    arrived = lax.ppermute(responses[-1], "tm", first_hop)
+    begin = lax.dynamic_slice_in_dim(arrived[0], member * cols, cols, 0)
+    begin = jnp.where(group == 1, begin, 0.0)
+    source_group = jnp.arange(time_parts * col_parts).reshape(-1, 1, 1) // members
+    for turn in range(1, groups - 1):
+        partial = jnp.sum(panels[-1] * begin[:, None], axis=0)
+        partial = partial + jnp.where(member == 0, responses[-1, 0], 0.0)
+        outgoing = jnp.broadcast_to(partial.reshape(1, members, 1, cols), (groups, members, 1, cols)).reshape(-1, 1, cols)
+        incoming = lax.all_to_all(outgoing, ("tm", "col"), 0, 0, tiled=True)
+        summed = jnp.sum(jnp.where(source_group == group - 1, incoming, 0.0), axis=(0, 1))
+        begin = jnp.where(group == turn + 1, summed, begin)
 
-    arrived = lax.ppermute(response[-1], "tm", [(i, (i + span) % time_parts) for i in range(time_parts)])
-    begin = jnp.where(group == 1, own_cols(arrived), 0.0)
-    for turn in range(1, groups - 1):
-        partial = jnp.sum(panels[-1, :cols, :] * begin[:, None], axis=0)
-        partial = partial + jnp.where(member == 0, 1.0, 0.0) * response[-1]
-        outgoing = jnp.zeros((time_parts * col_parts, cols), full)
-        outgoing = lax.dynamic_update_slice_in_dim(outgoing, partial.reshape(members, cols), ((group + 1) % groups) * members, 0)
-        incoming = lax.all_to_all(outgoing, ("tm", "col"), 0, 0)
-        begin = jnp.where(group == turn + 1, jnp.sum(incoming, axis=0), begin)
-
-    partials = jnp.sum(panels[:, :cols, :] * begin[None, :, None], axis=1)
-    received = lax.all_to_all(partials, "tm", 0, 0, axis_index_groups=teams)
+    partials = jnp.sum(panels * begin[None, :, None], axis=1)[:, None, :]
+    received = lax.all_to_all(partials, "tm", 0, 0, axis_index_groups=teams, tiled=True)
     summed = jnp.sum(received, axis=0).reshape(col_parts, state_size // col_parts)
     slab_end = lax.psum_scatter(summed, "col", scatter_dimension=0) if col_parts != 2 else (
         lax.dynamic_index_in_dim(summed, col_index, 0, False)
         + lax.ppermute(lax.dynamic_index_in_dim(summed, 1 - col_index, 0, False), "col", [(0, 1), (1, 0)])
     )
-    own_response = lax.dynamic_index_in_dim(response, slab, 0, False).reshape(col_parts, -1)
+    own_response = lax.dynamic_index_in_dim(responses, slab, 0, False).reshape(col_parts, -1)
     slab_end = slab_end + lax.dynamic_index_in_dim(own_response, col_index, 0, False)
     return slab_end[None, :]
 

time: 100 us -> 98.4 us (0.984)
  blocking collectives: 10.1 us -> 0 us
  starting transfers between devices: 9.89 us -> 19.4 us
  waiting for transfers between devices: 23 us -> 25.9 us
  local copies, waits for them, and re-layouts: 5.04 us -> 2.67 us
  other arithmetic: 7.79 us -> 6.5 us
    all_to_all x1 -> x0, blocking collectives: 10.1 us -> none  [shards(): lax.all_to_all(jnp.broadcast_to(own, (span,) + own.shape), 'tm', 0, 0, ax...]
    ppermute x1 -> x3, starting transfers between devices: 1.57 us -> 7.29 us  [the longest x2 5.15 us: team_gather(): lax.ppermute(value, 'tm', [(i, i ^ step) for i in range(lax.axis_size('tm...]
    all_to_all x3, starting transfers between devices: 8.25 us -> 12.1 us  [the longest x2 8.85 us: shards(): incoming = lax.all_to_all(outgoing, ('tm', 'col'), 0, 0, tiled=True)]
    dynamic_update_slice x2 -> x0, other arithmetic: 2.72 us -> none  [shards(): lax.dynamic_update_slice_in_dim(outgoing, partial.reshape(members, cols),...]
    ppermute x1 -> x3, waiting for transfers between devices: 3.84 us -> 5.73 us  [the longest x2 4.14 us: team_gather(): lax.ppermute(value, 'tm', [(i, i ^ step) for i in range(lax.axis_size('tm...]
    all_to_all x3 -> x0, local copies, waits for them, and re-layouts: 1.82 us -> none  [the longest x2 1.21 us: shards(): incoming = lax.all_to_all(outgoing, ('tm', 'col'), 0, 0)]
    broadcast_in_dim x1 -> x3, local copies, waits for them, and re-layouts: 0.01 us -> 1.8 us  [the longest x2 1.19 us: shards(): jnp.broadcast_to(partial.reshape(1, members, 1, cols), (groups, members,...]
    slice x2 -> x0, local copies, waits for them, and re-layouts: 1.68 us -> none  [the longest x1 0.92 us: shards(): response = panels[:, -1, :]]
  transfers between devices with their start and end apart: 5 -> 7, of which waited for: 5 -> 7; matrix products, arithmetic and copies ran while one was open for 1% -> 0% of each run, Pallas kernels for 0% -> 0%
where the time goes in v3:
time: 98.4 us; the launch traced here: 97.9 us
  Pallas kernels  43.3 us (44%)
  waiting for transfers between devices  25.9 us (26%)
  starting transfers between devices  19.4 us (20%)
  other arithmetic  6.5 us (7%)
  local copies, waits for them, and re-layouts  2.67 us (3%)
    pallas_call x1, Pallas kernels, shards(): panel_kernel(state_size, nodes, span, cols)  43.3 us
    all_to_all x2, waiting for transfers between devices, shards(): incoming = lax.all_to_all(outgoing, ('tm', 'col'), 0, 0, tiled=True)  14.3 us
    all_to_all x2, starting transfers between devices, shards(): incoming = lax.all_to_all(outgoing, ('tm', 'col'), 0, 0, tiled=True)  8.85 us
    ppermute x2, starting transfers between devices, team_gather(): lax.ppermute(value, 'tm', [(i, i ^ step) for i in range(lax.axis_size('tm...  5.15 us
    all_to_all x1, waiting for transfers between devices, shards(): lax.all_to_all(partials, 'tm', 0, 0, axis_index_groups=teams, tiled=True)  4.67 us
    ppermute x2, waiting for transfers between devices, team_gather(): lax.ppermute(value, 'tm', [(i, i ^ step) for i in range(lax.axis_size('tm...  4.14 us
    all_to_all x1, starting transfers between devices, shards(): lax.all_to_all(partials, 'tm', 0, 0, axis_index_groups=teams, tiled=True)  3.25 us
    reduce_sum x2, other arithmetic, shards(): partial = jnp.sum(panels[-1] * begin[:, None], axis=0)  2.3 us
  transfers between devices with their start and end apart: 7, of which 7 were waited for; matrix products, arithmetic and copies ran while one was open for 0% of the time, Pallas kernels for 0%

profile of v3, /device:TPU:0, one launch (start us, length us, event | category | flops | bytes accessed | tf_op | source)
XLA Modules:
  0.0 97.9 jit_solution(14791351020887451989)
XLA Ops:
  0.0 0.0 copy-start
  0.0 0.7 copy.10
  0.8 0.0 copy-done
  0.8 0.1 broadcast_bitcast_fusion
  0.8 3.0 %collective-permute-start = (f32[1,6,1024]{2,1,0:T(8,128)S(1)}, f32[1,6,1024]{2,1,0:T(8,128)S(1)}, u32[]{:S(2)}, u32[]{:S(2)}) collective-permute-start(f32[1,6,1024]{2,1,0:T(8,128)S(1)} %maximum_bitcast_fusion), channel_id=1, source_target_pairs={{0,2},{2,0},{4,6},{6,4},{8,10},{10,8},{12,14},{14,12},{16,18},{18,... | collective-permute-start | bytes 73736 | tf_op jit(solution)/shard_map/ppermute | solution.py:118
  3.9 1.9 %collective-permute-done = f32[1,6,1024]{2,1,0:T(8,128)S(1)} collective-permute-done((f32[1,6,1024]{2,1,0:T(8,128)S(1)}, f32[1,6,1024]{2,1,0:T(8,128)S(1)}, u32[]{:S(2)}, u32[]{:S(2)}) %collective-permute-start) | collective-permute-done | bytes 24608 | tf_op jit(solution)/shard_map/ppermute | solution.py:118
  5.8 2.1 %collective-permute-start.1 = (f32[2,6,1024]{2,1,0:T(8,128)S(1)}, f32[2,6,1024]{2,1,0:T(8,128)S(1)}, u32[]{:S(2)}, u32[]{:S(2)}) collective-permute-start(f32[2,6,1024]{2,1,0:T(8,128)S(1)} %pad_maximum_fusion.1), channel_id=1, source_target_pairs={{0,4},{2,6},{4,0},{6,2},{8,12},{10,14},{12,8},{14,10},{16,20},{18,... | collective-permute-start | bytes 147464 | tf_op jit(solution)/shard_map/ppermute | solution.py:118
  7.9 2.2 %collective-permute-done.1 = f32[2,6,1024]{2,1,0:T(8,128)S(1)} collective-permute-done((f32[2,6,1024]{2,1,0:T(8,128)S(1)}, f32[2,6,1024]{2,1,0:T(8,128)S(1)}, u32[]{:S(2)}, u32[]{:S(2)}) %collective-permute-start.1) | collective-permute-done | bytes 49184 | tf_op jit(solution)/shard_map/ppermute | solution.py:118
  10.2 0.7 pad_maximum_fusion.slab_data
  10.9 43.3 %shard_map.55 = (f32[4,128,1024]{2,1,0:T(8,128)}, f32[4,1,1024]{2,1,0:T(1,128)}) custom-call(f32[1024,1024]{1,0:T(8,128)} %coupling.1, f32[1024,1024]{1,0:T(8,128)} %modulation.1, f32[1,1024]{1,0:T(1,128)} %bitcast.49, f32[4,6,1024]{2,1,0:T(8,128)} %pad_maximum_fusion.slab_data), custom_call_target="tpu_custom_call" | custom-call | tf_op jit(solution)/shard_map/pallas_call | solution.py:143
  54.1 0.7 slice_bitcast_fusion
  54.8 2.1 %collective-permute-start.2 = (f32[1,1024]{1,0:T(1,128)S(1)}, f32[1,1024]{1,0:T(1,128)S(1)}, u32[]{:S(2)}, u32[]{:S(2)}) collective-permute-start(f32[1,1024]{1,0:T(1,128)S(1)} %get-tuple-element.13), channel_id=1, source_target_pairs={{0,8},{2,10},{4,12},{6,14},{8,0},{10,2},{12,4},{14,6},{16,24},{18,... | collective-permute-start | bytes 12296 | tf_op jit(solution)/shard_map/ppermute | solution.py:149
  57.0 1.6 %collective-permute-done.2 = f32[1,1024]{1,0:T(1,128)S(1)} collective-permute-done((f32[1,1024]{1,0:T(1,128)S(1)}, f32[1,1024]{1,0:T(1,128)S(1)}, u32[]{:S(2)}, u32[]{:S(2)}) %collective-permute-start.2) | collective-permute-done | bytes 4128 | tf_op jit(solution)/shard_map/ppermute | solution.py:149
  58.6 1.1 %fusion = f32[1024]{0:T(1024)S(1)} fusion(f32[4,128,1024]{2,1,0:T(8,128)} %get-tuple-element.7, f32[128]{0:T(128)S(1)} %fusion.2), kind=kLoop, calls=%fused_computation.3 | loop fusion | flops 261120 | bytes 528896 | tf_op jit(solution)/shard_map/reduce_sum | solution.py:154
  59.7 0.6 broadcast_in_dim.67
  60.3 6.4 %all-to-all-start = ((f32[32,1,128]{2,1,0:T(1,128)}), f32[32,1,128]{2,1,0:T(1,128)S(1)}, u32[]{:S(2)}, u32[]{:S(2)}) async-start(f32[32,1,128]{2,1,0:T(1,128)} %bitcast.10), calls=%async_computation | async-start | bytes 32768 | tf_op jit(solution)/shard_map/all_to_all | solution.py:157
  66.7 7.2 %all-to-all-done = f32[32,1,128]{2,1,0:T(1,128)S(1)} async-done(((f32[32,1,128]{2,1,0:T(1,128)}), f32[32,1,128]{2,1,0:T(1,128)S(1)}, u32[]{:S(2)}, u32[]{:S(2)}) %all-to-all-start) | async-done | bytes 16416 | tf_op jit(solution)/shard_map/all_to_all | solution.py:157
  73.9 0.1 broadcast_select_fusion.3
  74.0 1.1 %fusion.1 = f32[1024]{0:T(1024)S(1)} fusion(f32[4,128,1024]{2,1,0:T(8,128)} %get-tuple-element.7, f32[128]{0:T(128)S(1)} %broadcast_select_fusion.8), kind=kLoop, calls=%fused_computation.4 | loop fusion | flops 261120 | bytes 528896 | tf_op jit(solution)/shard_map/reduce_sum | solution.py:154
  75.2 0.6 broadcast_in_dim.70
  75.8 2.5 %all-to-all-start.1 = ((f32[32,1,128]{2,1,0:T(1,128)}), f32[32,1,128]{2,1,0:T(1,128)S(1)}, u32[]{:S(2)}, u32[]{:S(2)}) async-start(f32[32,1,128]{2,1,0:T(1,128)} %bitcast.13), calls=%async_computation.1 | async-start | bytes 32768 | tf_op jit(solution)/shard_map/all_to_all | solution.py:157
  78.3 7.2 %all-to-all-done.1 = f32[32,1,128]{2,1,0:T(1,128)S(1)} async-done(((f32[32,1,128]{2,1,0:T(1,128)}), f32[32,1,128]{2,1,0:T(1,128)S(1)}, u32[]{:S(2)}, u32[]{:S(2)}) %all-to-all-start.1) | async-done | bytes 16416 | tf_op jit(solution)/shard_map/all_to_all | solution.py:157
  85.5 0.1 broadcast_select_fusion.2
  85.6 1.9 %multiply_reduce_fusion = f32[4,1024]{1,0:T(4,128)S(1)} fusion(f32[4,128,1024]{2,1,0:T(8,128)} %get-tuple-element.7, f32[128]{0:T(128)S(1)} %broadcast_select_fusion.9), kind=kLoop, calls=%fused_computation | loop fusion | flops 1044480 | bytes 2114048 | tf_op jit(solution)/shard_map/reduce_sum | solution.py:161
  87.5 0.6 broadcast_in_dim.72
  88.1 3.2 %all-to-all-start.2 = ((f32[4,1,1024]{2,1,0:T(1,128)}), f32[4,1,1024]{2,1,0:T(1,128)S(1)}, u32[]{:S(2)}, u32[]{:S(2)}) async-start(f32[4,1,1024]{2,1,0:T(1,128)} %broadcast_in_dim.72), calls=%async_computation.2 | async-start | bytes 32768 | tf_op jit(solution)/shard_map/all_to_all | solution.py:162
  91.4 4.7 %all-to-all-done.2 = f32[4,1,1024]{2,1,0:T(1,128)S(1)} async-done(((f32[4,1,1024]{2,1,0:T(1,128)}), f32[4,1,1024]{2,1,0:T(1,128)S(1)}, u32[]{:S(2)}, u32[]{:S(2)}) %all-to-all-start.2) | async-done | bytes 16416 | tf_op jit(solution)/shard_map/all_to_all | solution.py:162
  96.1 0.1 collective-permute-start.3
  96.2 1.1 %collective-permute-done.3 = f32[512]{0:T(512)S(1)} collective-permute-done((f32[512]{0:T(512)S(1)}, f32[512]{0:T(512)S(1)}, u32[]{:S(2)}, u32[]{:S(2)}) %collective-permute-start.3) | collective-permute-done | bytes 2080 | tf_op jit(solution)/shard_map/ppermute | solution.py:166
  97.3 0.6 add_add_fusion
  (18 shorter events, 0.2 us)
Async XLA Ops:
  0.0 0.8 copy-start
  0.8 4.9 %collective-permute-start = (f32[1,6,1024]{2,1,0:T(8,128)S(1)}, f32[1,6,1024]{2,1,0:T(8,128)S(1)}, u32[]{:S(2)}, u32[]{:S(2)}) collective-permute-start(f32[1,6,1024]{2,1,0:T(8,128)S(1)} %maximum_bitcast_fusion), channel_id=1, source_target_pairs={{0,2},{2,0},{4,6},{6,4},{8,10},{10,8},{12,14},{14,12},{16,18},{18,... | collective-permute-start | bytes 73736 | tf_op jit(solution)/shard_map/ppermute | solution.py:118
  5.8 4.4 %collective-permute-start.1 = (f32[2,6,1024]{2,1,0:T(8,128)S(1)}, f32[2,6,1024]{2,1,0:T(8,128)S(1)}, u32[]{:S(2)}, u32[]{:S(2)}) collective-permute-start(f32[2,6,1024]{2,1,0:T(8,128)S(1)} %pad_maximum_fusion.1), channel_id=1, source_target_pairs={{0,4},{2,6},{4,0},{6,2},{8,12},{10,14},{12,8},{14,10},{16,20},{18,... | collective-permute-start | bytes 147464 | tf_op jit(solution)/shard_map/ppermute | solution.py:118
  54.8 3.7 %collective-permute-start.2 = (f32[1,1024]{1,0:T(1,128)S(1)}, f32[1,1024]{1,0:T(1,128)S(1)}, u32[]{:S(2)}, u32[]{:S(2)}) collective-permute-start(f32[1,1024]{1,0:T(1,128)S(1)} %get-tuple-element.13), channel_id=1, source_target_pairs={{0,8},{2,10},{4,12},{6,14},{8,0},{10,2},{12,4},{14,6},{16,24},{18,... | collective-permute-start | bytes 12296 | tf_op jit(solution)/shard_map/ppermute | solution.py:149
  60.3 13.5 %all-to-all-start = ((f32[32,1,128]{2,1,0:T(1,128)}), f32[32,1,128]{2,1,0:T(1,128)S(1)}, u32[]{:S(2)}, u32[]{:S(2)}) async-start(f32[32,1,128]{2,1,0:T(1,128)} %bitcast.10), calls=%async_computation | async-start | bytes 32768 | tf_op jit(solution)/shard_map/all_to_all | solution.py:157
  75.8 9.7 %all-to-all-start.1 = ((f32[32,1,128]{2,1,0:T(1,128)}), f32[32,1,128]{2,1,0:T(1,128)S(1)}, u32[]{:S(2)}, u32[]{:S(2)}) async-start(f32[32,1,128]{2,1,0:T(1,128)} %bitcast.13), calls=%async_computation.1 | async-start | bytes 32768 | tf_op jit(solution)/shard_map/all_to_all | solution.py:157
  88.1 7.9 %all-to-all-start.2 = ((f32[4,1,1024]{2,1,0:T(1,128)}), f32[4,1,1024]{2,1,0:T(1,128)S(1)}, u32[]{:S(2)}, u32[]{:S(2)}) async-start(f32[4,1,1024]{2,1,0:T(1,128)} %broadcast_in_dim.72), calls=%async_computation.2 | async-start | bytes 32768 | tf_op jit(solution)/shard_map/all_to_all | solution.py:162
  96.1 1.2 %collective-permute-start.3 = (f32[512]{0:T(512)S(1)}, f32[512]{0:T(512)S(1)}, u32[]{:S(2)}, u32[]{:S(2)}) collective-permute-start(f32[512]{0:T(512)S(1)} %bitcast.50), channel_id=1, source_target_pairs={{0,1},{1,0},{2,3},{3,2},{4,5},{5,4},{6,7},{7,6},{8,9},{9,8},{10,11... | collective-permute-start | bytes 6152 | tf_op jit(solution)/shard_map/ppermute | solution.py:166
